TPU v7x, 512 devices: a whole 4x8x8 slice. The times are simulated.
512 devices in a mesh: cols: 64 (over z, x, y_hi), rows: 8 (over y_lo, core).
Axes of the slice: x: 4, y: 8 (y_hi: 2, y_lo: 4; y = y_hi * 4 + y_lo), z: 8, core: 2. Of those that a mesh axis runs over, the one named last changes fastest.
Arguments:
- vectors: float32 [8192, 16384], P('rows', 'cols'), may hold values from -6 to 6
- reflectors: float32 [15, 1024, 512], P(None, None, 'cols'), may hold values from -40 to 40, as said below
- factors: float32 [15, 512, 512], P(None, None, 'cols'), may hold values from -1 to 1
Outputs:
- result: float32 [8192, 16384], P('rows', 'cols')
Inputs may be any that keep to these rules, and one draw needn't show every extreme that they name: `reflectors`: column j of each block is zero outside its rows j to j + 511, and its entry in row j is 1.
All inputs are finite; a program needn't handle non-finite values.
Results may differ from a plain program's by a relative error of at most 0.00028.
Values sent between devices are 32-bit elements; how exact they have to be, the bound alone decides.
A program may use at most 64 MiB of HBM per device.

v0:
```python
import jax
import jax.numpy as jnp
from jax import lax
from jax.sharding import PartitionSpec as P


def rows_first(arrays, axis, dims):
    turned = [jnp.moveaxis(a, dim, 0) for a, dim in zip(arrays, dims)]
    both = jnp.concatenate([t.reshape(len(t), -1) for t in turned], axis=1)
    filled, at, outs = (lax.all_gather(both, axis, axis=0, tiled=True), 0, [])
    for t, dim in zip(turned, dims):
        slab = filled[:, at : at + t[0].size].reshape(-1, *t.shape[1:])
        outs.append(jnp.moveaxis(slab, 0, dim))
        at += t[0].size
    return tuple(outs)


def shifted(value, axis, by):
    length = lax.axis_size(axis)
    pairs = [(i, i + by) for i in range(length) if 0 <= i + by < length]
    return lax.ppermute(value, axis, pairs)


def reflect(window, basis_cols, factor):
    highest = lax.Precision.HIGHEST
    weights = lax.dot_general(
        basis_cols,
        window,
        (((0,), (0,)), ((), ())),
        precision=highest,
        preferred_element_type=jnp.float32,
    )
    coeffs = jnp.dot(factor, weights, precision=highest, preferred_element_type=jnp.float32)
    return window - jnp.dot(
        basis_cols, coeffs, precision=highest, preferred_element_type=jnp.float32
    )


def body(vectors, reflectors, factors):
    row_count = lax.axis_size("rows")
    row_index = lax.axis_index("rows")
    rows_dev, cols_dev = vectors.shape
    half_rows = rows_dev // 2
    first_index = jnp.maximum(2 * row_index - 1, 0)
    own_index = 2 * row_index
    upper_basis = lax.dynamic_index_in_dim(reflectors, first_index, 0, keepdims=False)
    upper_factor = lax.dynamic_index_in_dim(factors, first_index, 0, keepdims=False)
    own_basis = lax.dynamic_index_in_dim(reflectors, own_index, 0, keepdims=False)
    own_factor = lax.dynamic_index_in_dim(factors, own_index, 0, keepdims=False)
    pair_basis = jnp.stack([upper_basis, own_basis])
    pair_factor = jnp.stack([upper_factor, own_factor])
    full_basis, full_factor = rows_first((pair_basis, pair_factor), "cols", (2, 2))
    upper_basis, own_basis = (full_basis[0], full_basis[1])
    upper_factor, own_factor = (full_factor[0], full_factor[1])
    stripe_count = 2
    stripe_cols = cols_dev // stripe_count
    has_upper = row_index > 0
    has_lower = row_index < row_count - 1

    def process(state_now, incoming, stripe_index):
        matrix, outgoing, returning = state_now
        start = stripe_index * stripe_cols
        stripe = lax.dynamic_slice_in_dim(matrix, start, stripe_cols, 1)
        window = reflect(
            jnp.concatenate([incoming, stripe[:half_rows]], 0), upper_basis, upper_factor
        )
        upper_rows = jnp.where(has_upper, window[half_rows:], stripe[:half_rows])
        stripe = reflect(
            jnp.concatenate([upper_rows, stripe[half_rows:]], 0), own_basis, own_factor
        )
        matrix = lax.dynamic_update_slice_in_dim(matrix, stripe, start, 1)
        return (matrix, stripe[half_rows:], window[:half_rows])

    def advance(turn_index, state_now):
        matrix, outgoing, returning = state_now
        incoming = shifted(outgoing, "rows", 1)
        arrived = shifted(returning, "rows", -1)
        late_stripe = turn_index - row_index - 2
        landing = (late_stripe >= 0) & (late_stripe < stripe_count) & has_lower
        late_start = jnp.clip(late_stripe, 0, stripe_count - 1) * stripe_cols
        current = lax.dynamic_slice(matrix, (half_rows, late_start), (half_rows, stripe_cols))
        matrix = lax.dynamic_update_slice(
            matrix, jnp.where(landing, arrived, current), (half_rows, late_start)
        )
        stripe_index = turn_index - row_index
        is_active = (stripe_index >= 0) & (stripe_index < stripe_count)
        safe_index = jnp.clip(stripe_index, 0, stripe_count - 1)

        def busy(state_in):
            return process(state_in, incoming, safe_index)

        def resting(state_in):
            return state_in

        return lax.cond(is_active, busy, resting, (matrix, outgoing, returning))

    blank = jnp.zeros((half_rows, stripe_cols), jnp.float32)
    matrix, outgoing, returning = lax.fori_loop(
        0, row_count + stripe_count, advance, (vectors, blank, blank)
    )
    return matrix


def solution(mesh):
    placed = (P("rows", "cols"), P(None, None, "cols"), P(None, None, "cols"))
    return jax.shard_map(
        body, mesh=mesh, in_specs=placed, out_specs=P("rows", "cols"), check_vma=False
    )
```

profile of v0, /device:TPU:25, one launch (start us, length us, event | category | flops | bytes accessed | tf_op | source)
XLA Modules:
  0.0 437.3 jit_solution(806147630762032506)
XLA Ops:
  8.8 2.6 copy.8
  11.3 166.3 %all-gather.2.cloned.1.call-done = f32[512,3072]{1,0:T(8,128)} async-done(((f32[8,3072]{1,0:T(8,128)}), f32[512,3072]{1,0:T(8,128)}) %all-gather.2.cloned.1.call-update) | async-done | bytes 6291472 | tf_op jit(solution)/shard_map/all_gather | solution.py:10
  177.6 4.8 %slice.43 = f32[512,2048]{1,0:T(8,128)} slice(f32[512,3072]{1,0:T(8,128)} %all-gather.2.cloned.1.call-done), slice={[0:512], [0:2048]} | slice | bytes 8388608 | tf_op jit(solution)/shard_map/slice | solution.py:12
  182.4 5.4 %copy.10 = f32[512,2048]{0,1:T(8,128)} copy(f32[512,2048]{1,0:T(8,128)} %slice.43) | data formatting | bytes 8388608 | tf_op jit(solution)/shard_map/reshape | solution.py:12
  187.8 3.2 slice.45
  190.9 1.9 copy.11
  195.4 1.8 slice_bitcast_fusion
  198.6 229.3 %while.19 = (s32[]{:T(128)}, f32[1024,256]{0,1:T(8,128)}, f32[512,128]{0,1:T(8,128)}, f32[512,128]{0,1:T(8,128)}, s32[]{:T(128)}, /*index=5*/pred[]{:T(512)}, pr...) while((s32[]{:T(128)}, f32[1024,256]{0,1:T(8,128)}, ...), condition=%wide.region_3.4_spmd, body=%wide.region_0.3_spmd.sunk | while | flops 4027449344 | bytes 42992328 | solution.py:98
  198.6 6.5 %collective-permute-start = (f32[512,128]{0,1:T(8,128)}, f32[512,128]{0,1:T(8,128)}, u32[]{:S(2)}, u32[]{:S(2)}) collective-permute-start(f32[512,128]{0,1:T(8,128)} %get-tuple-element.479), channel_id=1, source_target_pairs={{1,0},{2,1},{3,2},{4,3},{5,4},{6,5},{7,6},{9,8},{10,9},{11,10},{12... | collective-permute-start | bytes 786440 | tf_op jit(solution)/shard_map/while/body/eval_jaxpr/ppermute | solution.py:21
  208.2 2.4 collective-permute-done.1
  210.5 9.5 %collective-permute-start = (f32[512,128]{0,1:T(8,128)}, f32[512,128]{0,1:T(8,128)}, u32[]{:S(2)}, u32[]{:S(2)}) collective-permute-start(f32[512,128]{0,1:T(8,128)} %get-tuple-element.479), channel_id=1, source_target_pairs={{1,0},{2,1},{3,2},{4,3},{5,4},{6,5},{7,6},{9,8},{10,9},{11,10},{12... | collective-permute-start | bytes 786440 | tf_op jit(solution)/shard_map/while/body/eval_jaxpr/ppermute | solution.py:21
  223.7 6.3 %collective-permute-start = (f32[512,128]{0,1:T(8,128)}, f32[512,128]{0,1:T(8,128)}, u32[]{:S(2)}, u32[]{:S(2)}) collective-permute-start(f32[512,128]{0,1:T(8,128)} %get-tuple-element.479), channel_id=1, source_target_pairs={{1,0},{2,1},{3,2},{4,3},{5,4},{6,5},{7,6},{9,8},{10,9},{11,10},{12... | collective-permute-start | bytes 786440 | tf_op jit(solution)/shard_map/while/body/eval_jaxpr/ppermute | solution.py:21
  233.6 6.2 %collective-permute-start = (f32[512,128]{0,1:T(8,128)}, f32[512,128]{0,1:T(8,128)}, u32[]{:S(2)}, u32[]{:S(2)}) collective-permute-start(f32[512,128]{0,1:T(8,128)} %get-tuple-element.479), channel_id=1, source_target_pairs={{1,0},{2,1},{3,2},{4,3},{5,4},{6,5},{7,6},{9,8},{10,9},{11,10},{12... | collective-permute-start | bytes 786440 | tf_op jit(solution)/shard_map/while/body/eval_jaxpr/ppermute | solution.py:21
  243.4 16.8 %collective-permute-start = (f32[512,128]{0,1:T(8,128)}, f32[512,128]{0,1:T(8,128)}, u32[]{:S(2)}, u32[]{:S(2)}) collective-permute-start(f32[512,128]{0,1:T(8,128)} %get-tuple-element.479), channel_id=1, source_target_pairs={{1,0},{2,1},{3,2},{4,3},{5,4},{6,5},{7,6},{9,8},{10,9},{11,10},{12... | collective-permute-start | bytes 786440 | tf_op jit(solution)/shard_map/while/body/eval_jaxpr/ppermute | solution.py:21
  263.2 7.7 %collective-permute-done.1 = f32[512,128]{0,1:T(8,128)S(1)} collective-permute-done((f32[512,128]{0,1:T(8,128)}, f32[512,128]{0,1:T(8,128)S(1)}, u32[]{:S(2)}, u32[]{:S(2)}) %collective-permute-start.1) | collective-permute-done | bytes 262176 | tf_op jit(solution)/shard_map/while/body/eval_jaxpr/ppermute | solution.py:21
  270.9 28.4 %collective-permute-start = (f32[512,128]{0,1:T(8,128)}, f32[512,128]{0,1:T(8,128)}, u32[]{:S(2)}, u32[]{:S(2)}) collective-permute-start(f32[512,128]{0,1:T(8,128)} %get-tuple-element.479), channel_id=1, source_target_pairs={{1,0},{2,1},{3,2},{4,3},{5,4},{6,5},{7,6},{9,8},{10,9},{11,10},{12... | collective-permute-start | bytes 786440 | tf_op jit(solution)/shard_map/while/body/eval_jaxpr/ppermute | solution.py:21
  302.4 10.7 %collective-permute-done.1 = f32[512,128]{0,1:T(8,128)S(1)} collective-permute-done((f32[512,128]{0,1:T(8,128)}, f32[512,128]{0,1:T(8,128)S(1)}, u32[]{:S(2)}, u32[]{:S(2)}) %collective-permute-start.1) | collective-permute-done | bytes 262176 | tf_op jit(solution)/shard_map/while/body/eval_jaxpr/ppermute | solution.py:21
  313.1 26.0 %collective-permute-start = (f32[512,128]{0,1:T(8,128)}, f32[512,128]{0,1:T(8,128)}, u32[]{:S(2)}, u32[]{:S(2)}) collective-permute-start(f32[512,128]{0,1:T(8,128)} %get-tuple-element.479), channel_id=1, source_target_pairs={{1,0},{2,1},{3,2},{4,3},{5,4},{6,5},{7,6},{9,8},{10,9},{11,10},{12... | collective-permute-start | bytes 786440 | tf_op jit(solution)/shard_map/while/body/eval_jaxpr/ppermute | solution.py:21
  340.4 1.7 select_dynamic-update-slice_fusion.2
  342.1 13.7 %collective-permute-done.1 = f32[512,128]{0,1:T(8,128)S(1)} collective-permute-done((f32[512,128]{0,1:T(8,128)}, f32[512,128]{0,1:T(8,128)S(1)}, u32[]{:S(2)}, u32[]{:S(2)}) %collective-permute-start.1) | collective-permute-done | bytes 262176 | tf_op jit(solution)/shard_map/while/body/eval_jaxpr/ppermute | solution.py:21
  355.9 23.0 %collective-permute-start = (f32[512,128]{0,1:T(8,128)}, f32[512,128]{0,1:T(8,128)}, u32[]{:S(2)}, u32[]{:S(2)}) collective-permute-start(f32[512,128]{0,1:T(8,128)} %get-tuple-element.479), channel_id=1, source_target_pairs={{1,0},{2,1},{3,2},{4,3},{5,4},{6,5},{7,6},{9,8},{10,9},{11,10},{12... | collective-permute-start | bytes 786440 | tf_op jit(solution)/shard_map/while/body/eval_jaxpr/ppermute | solution.py:21
  382.5 15.0 %conditional.2 = ((f32[1024,256]{0,1:T(8,128)}, f32[512,128]{0,1:T(8,128)}, f32[512,128]{0,1:T(8,128)})) conditional(s32[]{:T(128)} %convert_element_type.11, (f32[1024,256]{0,1:T(8,128)}, f32[512,128]{0,1:T(8,128)}, f32[512,128]{0,1:T(8,128)}) %tuple.54, (pred[]{:T(512)}, s32[]{:T(128)}, f32[1024,256]{0,1:T(8,128)}, f32[512,128]{0,1:T(8,128)S(1)}, ...), branch_computations={%region_1.1_spmd, %region_2.2_spmd} | conditional | flops 4027383808 | bytes 40108272 | solution.py:95
  383.7 3.0 fusion.3
  387.9 2.3 fusion
  393.5 2.3 constant_dynamic-update-slice_fusion
  397.5 6.2 %collective-permute-start = (f32[512,128]{0,1:T(8,128)}, f32[512,128]{0,1:T(8,128)}, u32[]{:S(2)}, u32[]{:S(2)}) collective-permute-start(f32[512,128]{0,1:T(8,128)} %get-tuple-element.479), channel_id=1, source_target_pairs={{1,0},{2,1},{3,2},{4,3},{5,4},{6,5},{7,6},{9,8},{10,9},{11,10},{12... | collective-permute-start | bytes 786440 | tf_op jit(solution)/shard_map/while/body/eval_jaxpr/ppermute | solution.py:21
  407.3 15.0 %conditional.2 = ((f32[1024,256]{0,1:T(8,128)}, f32[512,128]{0,1:T(8,128)}, f32[512,128]{0,1:T(8,128)})) conditional(s32[]{:T(128)} %convert_element_type.11, (f32[1024,256]{0,1:T(8,128)}, f32[512,128]{0,1:T(8,128)}, f32[512,128]{0,1:T(8,128)}) %tuple.54, (pred[]{:T(512)}, s32[]{:T(128)}, f32[1024,256]{0,1:T(8,128)}, f32[512,128]{0,1:T(8,128)S(1)}, ...), branch_computations={%region_1.1_spmd, %region_2.2_spmd} | conditional | flops 4027383808 | bytes 40108272 | solution.py:95
  408.5 3.0 fusion.3
  412.7 2.3 fusion
  418.3 2.3 constant_dynamic-update-slice_fusion
  422.3 2.0 collective-permute-start
  428.0 2.5 copy.9
  (83 shorter events, 52.5 us)
Async XLA Ops:
  6.5 171.1 %all-gather.2.cloned.1.call-start = ((), (), s32[]{:S(2)}) async-start(), calls=%async_computation | async-start | bytes 6389760 | tf_op jit(solution)/shard_map/all_gather | solution.py:10
  192.9 2.6 copy-start.4
  198.6 7.8 %collective-permute-start = (f32[512,128]{0,1:T(8,128)}, f32[512,128]{0,1:T(8,128)}, u32[]{:S(2)}, u32[]{:S(2)}) collective-permute-start(f32[512,128]{0,1:T(8,128)} %get-tuple-element.479), channel_id=1, source_target_pairs={{1,0},{2,1},{3,2},{4,3},{5,4},{6,5},{7,6},{9,8},{10,9},{11,10},{12... | collective-permute-start | bytes 786440 | tf_op jit(solution)/shard_map/while/body/eval_jaxpr/ppermute | solution.py:21
  205.1 5.4 %collective-permute-start.1 = (f32[512,128]{0,1:T(8,128)}, f32[512,128]{0,1:T(8,128)S(1)}, u32[]{:S(2)}, u32[]{:S(2)}) collective-permute-start(f32[512,128]{0,1:T(8,128)} %get-tuple-element.478), channel_id=1, source_target_pairs={{0,1},{1,2},{2,3},{3,4},{4,5},{5,6},{6,7},{8,9},{9,10},{10,11},{11... | collective-permute-start | bytes 786440 | tf_op jit(solution)/shard_map/while/body/eval_jaxpr/ppermute | solution.py:21
  210.5 10.8 %collective-permute-start = (f32[512,128]{0,1:T(8,128)}, f32[512,128]{0,1:T(8,128)}, u32[]{:S(2)}, u32[]{:S(2)}) collective-permute-start(f32[512,128]{0,1:T(8,128)} %get-tuple-element.479), channel_id=1, source_target_pairs={{1,0},{2,1},{3,2},{4,3},{5,4},{6,5},{7,6},{9,8},{10,9},{11,10},{12... | collective-permute-start | bytes 786440 | tf_op jit(solution)/shard_map/while/body/eval_jaxpr/ppermute | solution.py:21
  220.0 3.6 collective-permute-start.1
  223.7 7.6 %collective-permute-start = (f32[512,128]{0,1:T(8,128)}, f32[512,128]{0,1:T(8,128)}, u32[]{:S(2)}, u32[]{:S(2)}) collective-permute-start(f32[512,128]{0,1:T(8,128)} %get-tuple-element.479), channel_id=1, source_target_pairs={{1,0},{2,1},{3,2},{4,3},{5,4},{6,5},{7,6},{9,8},{10,9},{11,10},{12... | collective-permute-start | bytes 786440 | tf_op jit(solution)/shard_map/while/body/eval_jaxpr/ppermute | solution.py:21
  230.0 3.6 collective-permute-start.1
  233.6 7.5 %collective-permute-start = (f32[512,128]{0,1:T(8,128)}, f32[512,128]{0,1:T(8,128)}, u32[]{:S(2)}, u32[]{:S(2)}) collective-permute-start(f32[512,128]{0,1:T(8,128)} %get-tuple-element.479), channel_id=1, source_target_pairs={{1,0},{2,1},{3,2},{4,3},{5,4},{6,5},{7,6},{9,8},{10,9},{11,10},{12... | collective-permute-start | bytes 786440 | tf_op jit(solution)/shard_map/while/body/eval_jaxpr/ppermute | solution.py:21
  239.8 3.6 collective-permute-start.1
  243.4 18.1 %collective-permute-start = (f32[512,128]{0,1:T(8,128)}, f32[512,128]{0,1:T(8,128)}, u32[]{:S(2)}, u32[]{:S(2)}) collective-permute-start(f32[512,128]{0,1:T(8,128)} %get-tuple-element.479), channel_id=1, source_target_pairs={{1,0},{2,1},{3,2},{4,3},{5,4},{6,5},{7,6},{9,8},{10,9},{11,10},{12... | collective-permute-start | bytes 786440 | tf_op jit(solution)/shard_map/while/body/eval_jaxpr/ppermute | solution.py:21
  260.2 10.7 %collective-permute-start.1 = (f32[512,128]{0,1:T(8,128)}, f32[512,128]{0,1:T(8,128)S(1)}, u32[]{:S(2)}, u32[]{:S(2)}) collective-permute-start(f32[512,128]{0,1:T(8,128)} %get-tuple-element.478), channel_id=1, source_target_pairs={{0,1},{1,2},{2,3},{3,4},{4,5},{5,6},{6,7},{8,9},{9,10},{10,11},{11... | collective-permute-start | bytes 786440 | tf_op jit(solution)/shard_map/while/body/eval_jaxpr/ppermute | solution.py:21
  270.9 29.7 %collective-permute-start = (f32[512,128]{0,1:T(8,128)}, f32[512,128]{0,1:T(8,128)}, u32[]{:S(2)}, u32[]{:S(2)}) collective-permute-start(f32[512,128]{0,1:T(8,128)} %get-tuple-element.479), channel_id=1, source_target_pairs={{1,0},{2,1},{3,2},{4,3},{5,4},{6,5},{7,6},{9,8},{10,9},{11,10},{12... | collective-permute-start | bytes 786440 | tf_op jit(solution)/shard_map/while/body/eval_jaxpr/ppermute | solution.py:21
  299.3 13.8 %collective-permute-start.1 = (f32[512,128]{0,1:T(8,128)}, f32[512,128]{0,1:T(8,128)S(1)}, u32[]{:S(2)}, u32[]{:S(2)}) collective-permute-start(f32[512,128]{0,1:T(8,128)} %get-tuple-element.478), channel_id=1, source_target_pairs={{0,1},{1,2},{2,3},{3,4},{4,5},{5,6},{6,7},{8,9},{9,10},{10,11},{11... | collective-permute-start | bytes 786440 | tf_op jit(solution)/shard_map/while/body/eval_jaxpr/ppermute | solution.py:21
  313.1 27.4 %collective-permute-start = (f32[512,128]{0,1:T(8,128)}, f32[512,128]{0,1:T(8,128)}, u32[]{:S(2)}, u32[]{:S(2)}) collective-permute-start(f32[512,128]{0,1:T(8,128)} %get-tuple-element.479), channel_id=1, source_target_pairs={{1,0},{2,1},{3,2},{4,3},{5,4},{6,5},{7,6},{9,8},{10,9},{11,10},{12... | collective-permute-start | bytes 786440 | tf_op jit(solution)/shard_map/while/body/eval_jaxpr/ppermute | solution.py:21
  339.1 16.8 %collective-permute-start.1 = (f32[512,128]{0,1:T(8,128)}, f32[512,128]{0,1:T(8,128)S(1)}, u32[]{:S(2)}, u32[]{:S(2)}) collective-permute-start(f32[512,128]{0,1:T(8,128)} %get-tuple-element.478), channel_id=1, source_target_pairs={{0,1},{1,2},{2,3},{3,4},{4,5},{5,6},{6,7},{8,9},{9,10},{10,11},{11... | collective-permute-start | bytes 786440 | tf_op jit(solution)/shard_map/while/body/eval_jaxpr/ppermute | solution.py:21
  355.9 24.3 %collective-permute-start = (f32[512,128]{0,1:T(8,128)}, f32[512,128]{0,1:T(8,128)}, u32[]{:S(2)}, u32[]{:S(2)}) collective-permute-start(f32[512,128]{0,1:T(8,128)} %get-tuple-element.479), channel_id=1, source_target_pairs={{1,0},{2,1},{3,2},{4,3},{5,4},{6,5},{7,6},{9,8},{10,9},{11,10},{12... | collective-permute-start | bytes 786440 | tf_op jit(solution)/shard_map/while/body/eval_jaxpr/ppermute | solution.py:21
  378.9 3.6 collective-permute-start.1
  382.5 4.2 copy-start.1
  383.7 4.2 copy-start
  391.0 2.5 copy-start.2
  395.8 1.0 copy-start.3
  397.5 7.5 %collective-permute-start = (f32[512,128]{0,1:T(8,128)}, f32[512,128]{0,1:T(8,128)}, u32[]{:S(2)}, u32[]{:S(2)}) collective-permute-start(f32[512,128]{0,1:T(8,128)} %get-tuple-element.479), channel_id=1, source_target_pairs={{1,0},{2,1},{3,2},{4,3},{5,4},{6,5},{7,6},{9,8},{10,9},{11,10},{12... | collective-permute-start | bytes 786440 | tf_op jit(solution)/shard_map/while/body/eval_jaxpr/ppermute | solution.py:21
  403.7 3.6 collective-permute-start.1
  407.3 4.2 copy-start.1
  408.5 4.2 copy-start
  415.8 2.5 copy-start.2
  420.6 1.0 copy-start.3
  422.3 3.3 collective-permute-start
  424.3 3.6 collective-permute-start.1
Sparse Core Ops, SparseCore 0:
  11.9 165.7 all-gather.1
where the time goes:
time: 439 us; the launch traced here: 437 us
  waiting for transfers between devices  204 us (46%)
  starting transfers between devices  144 us (33%)
  local copies, waits for them, and re-layouts  33.4 us (8%)
  matrix products  22.5 us (5%)
  other arithmetic  19.3 us (4%)
  between operations  13.4 us (3%)
    all_gather x1, waiting for transfers between devices, rows_first(): filled, at, outs = (lax.all_gather(both, axis, axis=0, tiled=True), 0, [])  166 us
    ppermute x20, starting transfers between devices, shifted(): return lax.ppermute(value, axis, pairs)  144 us
    ppermute x20, waiting for transfers between devices, shifted(): return lax.ppermute(value, axis, pairs)  38.1 us
    dynamic_update_slice x10, other arithmetic, advance(): lax.dynamic_update_slice(matrix, jnp.where(landing, arrived, current), (h...  17.1 us
    dot_general x4, matrix products, reflect(): jnp.dot(basis_cols, coeffs, precision=highest, preferred_element_type=jnp...  9.19 us
  transfers between devices with their start and end apart: 21, of which 11 were waited for; matrix products, arithmetic and copies ran while one was open for 5% of the time, Pallas kernels for 0%

commit v1 on v0

--- a/solution.py
+++ b/solution.py
@@ -2,12 +2,17 @@
 import jax.numpy as jnp
 from jax import lax
 from jax.sharding import PartitionSpec as P
+from jax.lax import all_to_all, psum
 
 
 def rows_first(arrays, axis, dims):
     turned = [jnp.moveaxis(a, dim, 0) for a, dim in zip(arrays, dims)]
     both = jnp.concatenate([t.reshape(len(t), -1) for t in turned], axis=1)
-    filled, at, outs = (lax.all_gather(both, axis, axis=0, tiled=True), 0, [])
+    filled, at, outs = (
+        jnp.concatenate(all_to_all(jnp.stack([both] * psum(1, axis)), axis, 0, 0), axis=0),
+        0,
+        [],
+    )
     for t, dim in zip(turned, dims):
         slab = filled[:, at : at + t[0].size].reshape(-1, *t.shape[1:])
         outs.append(jnp.moveaxis(slab, 0, dim))

time: 439 us -> 424 us (0.966)
  the two profiles are of different devices: /device:TPU:25 before, /device:TPU:121 now
where the time goes in v1:
time: 424 us; the launch traced here: 423 us
  waiting for transfers between devices  198 us (47%)
  starting transfers between devices  149 us (35%)
  local copies, waits for them, and re-layouts  34.4 us (8%)
  matrix products  22.6 us (5%)
  other arithmetic  18.8 us (4%)
    all_to_all x1, waiting for transfers between devices, rows_first(): all_to_all(jnp.stack([both] * psum(1, axis)), axis, 0, 0)  151 us
    ppermute x20, starting transfers between devices, shifted(): return lax.ppermute(value, axis, pairs)  131 us
    ppermute x20, waiting for transfers between devices, shifted(): return lax.ppermute(value, axis, pairs)  46.3 us
    all_to_all x1, starting transfers between devices, rows_first(): all_to_all(jnp.stack([both] * psum(1, axis)), axis, 0, 0)  17.5 us
    dynamic_update_slice x10, other arithmetic, advance(): lax.dynamic_update_slice(matrix, jnp.where(landing, arrived, current), (h...  17.3 us
    dot_general x4, matrix products, reflect(): jnp.dot(basis_cols, coeffs, precision=highest, preferred_element_type=jnp...  9.19 us
    dot_general x4, matrix products, reflect(): lax.dot_general(basis_cols, window, (((0,), (0,)), ((), ())), precision=h...  8.65 us
  transfers between devices with their start and end apart: 21, of which 11 were waited for; matrix products, arithmetic and copies ran while one was open for 4% of the time, Pallas kernels for 0%

profile of v1, /device:TPU:121, one launch (start us, length us, event | category | flops | bytes accessed | tf_op | source)
XLA Modules:
  0.0 423.0 jit_solution(5365069694602691470)
XLA Ops:
  1.6 3.4 stack.8
  4.9 17.5 %all-to-all-start = ((f32[64,8,3072]{2,1,0:T(8,128)}), f32[64,8,3072]{2,1,0:T(8,128)}, u32[]{:S(2)}, u32[]{:S(2)}) async-start(f32[64,8,3072]{2,1,0:T(8,128)} %stack.8), calls=%async_computation | async-start | bytes 12582912 | tf_op jit(solution)/shard_map/all_to_all | solution.py:12
  23.8 151.5 %all-to-all-done = f32[64,8,3072]{2,1,0:T(8,128)} async-done(((f32[64,8,3072]{2,1,0:T(8,128)}), f32[64,8,3072]{2,1,0:T(8,128)}, u32[]{:S(2)}, u32[]{:S(2)}) %all-to-all-start) | async-done | bytes 6291488 | tf_op jit(solution)/shard_map/all_to_all | solution.py:12
  175.3 1.8 slice.45
  177.2 4.7 %slice.43 = f32[512,2048]{1,0:T(8,128)} slice(f32[512,3072]{1,0:T(8,128)} %bitcast.6), slice={[0:512], [0:2048]} | slice | bytes 8388608 | tf_op jit(solution)/shard_map/slice | solution.py:17
  181.9 5.4 %copy.10 = f32[512,2048]{0,1:T(8,128)} copy(f32[512,2048]{1,0:T(8,128)} %slice.43) | data formatting | bytes 8388608 | tf_op jit(solution)/shard_map/reshape | solution.py:17
  187.3 1.8 copy.11
  189.1 2.8 slice_bitcast_fusion.2
  195.2 225.3 %while.19 = (s32[]{:T(128)}, f32[1024,256]{0,1:T(8,128)}, f32[512,128]{0,1:T(8,128)}, f32[512,128]{0,1:T(8,128)}, s32[]{:T(128)}, /*index=5*/pred[]{:T(512)}, pr...) while((s32[]{:T(128)}, f32[1024,256]{0,1:T(8,128)}, ...), condition=%wide.region_3.4_spmd, body=%wide.region_0.3_spmd.sunk | while | flops 4027449344 | bytes 42992328 | solution.py:103
  195.2 3.6 collective-permute-start
  202.4 6.2 %collective-permute-start = (f32[512,128]{0,1:T(8,128)}, f32[512,128]{0,1:T(8,128)}, u32[]{:S(2)}, u32[]{:S(2)}) collective-permute-start(f32[512,128]{0,1:T(8,128)} %get-tuple-element.479), channel_id=1, source_target_pairs={{1,0},{2,1},{3,2},{4,3},{5,4},{6,5},{7,6},{9,8},{10,9},{11,10},{12... | collective-permute-start | bytes 786440 | tf_op jit(solution)/shard_map/while/body/eval_jaxpr/ppermute | solution.py:26
  211.7 11.0 %collective-permute-done.1 = f32[512,128]{0,1:T(8,128)S(1)} collective-permute-done((f32[512,128]{0,1:T(8,128)}, f32[512,128]{0,1:T(8,128)S(1)}, u32[]{:S(2)}, u32[]{:S(2)}) %collective-permute-start.1) | collective-permute-done | bytes 262176 | tf_op jit(solution)/shard_map/while/body/eval_jaxpr/ppermute | solution.py:26
  222.7 10.4 %collective-permute-start = (f32[512,128]{0,1:T(8,128)}, f32[512,128]{0,1:T(8,128)}, u32[]{:S(2)}, u32[]{:S(2)}) collective-permute-start(f32[512,128]{0,1:T(8,128)} %get-tuple-element.479), channel_id=1, source_target_pairs={{1,0},{2,1},{3,2},{4,3},{5,4},{6,5},{7,6},{9,8},{10,9},{11,10},{12... | collective-permute-start | bytes 786440 | tf_op jit(solution)/shard_map/while/body/eval_jaxpr/ppermute | solution.py:26
  236.7 6.3 %collective-permute-start = (f32[512,128]{0,1:T(8,128)}, f32[512,128]{0,1:T(8,128)}, u32[]{:S(2)}, u32[]{:S(2)}) collective-permute-start(f32[512,128]{0,1:T(8,128)} %get-tuple-element.479), channel_id=1, source_target_pairs={{1,0},{2,1},{3,2},{4,3},{5,4},{6,5},{7,6},{9,8},{10,9},{11,10},{12... | collective-permute-start | bytes 786440 | tf_op jit(solution)/shard_map/while/body/eval_jaxpr/ppermute | solution.py:26
  246.7 6.3 %collective-permute-start = (f32[512,128]{0,1:T(8,128)}, f32[512,128]{0,1:T(8,128)}, u32[]{:S(2)}, u32[]{:S(2)}) collective-permute-start(f32[512,128]{0,1:T(8,128)} %get-tuple-element.479), channel_id=1, source_target_pairs={{1,0},{2,1},{3,2},{4,3},{5,4},{6,5},{7,6},{9,8},{10,9},{11,10},{12... | collective-permute-start | bytes 786440 | tf_op jit(solution)/shard_map/while/body/eval_jaxpr/ppermute | solution.py:26
  256.0 7.3 %collective-permute-done.1 = f32[512,128]{0,1:T(8,128)S(1)} collective-permute-done((f32[512,128]{0,1:T(8,128)}, f32[512,128]{0,1:T(8,128)S(1)}, u32[]{:S(2)}, u32[]{:S(2)}) %collective-permute-start.1) | collective-permute-done | bytes 262176 | tf_op jit(solution)/shard_map/while/body/eval_jaxpr/ppermute | solution.py:26
  263.3 28.4 %collective-permute-start = (f32[512,128]{0,1:T(8,128)}, f32[512,128]{0,1:T(8,128)}, u32[]{:S(2)}, u32[]{:S(2)}) collective-permute-start(f32[512,128]{0,1:T(8,128)} %get-tuple-element.479), channel_id=1, source_target_pairs={{1,0},{2,1},{3,2},{4,3},{5,4},{6,5},{7,6},{9,8},{10,9},{11,10},{12... | collective-permute-start | bytes 786440 | tf_op jit(solution)/shard_map/while/body/eval_jaxpr/ppermute | solution.py:26
  294.8 10.7 %collective-permute-done.1 = f32[512,128]{0,1:T(8,128)S(1)} collective-permute-done((f32[512,128]{0,1:T(8,128)}, f32[512,128]{0,1:T(8,128)S(1)}, u32[]{:S(2)}, u32[]{:S(2)}) %collective-permute-start.1) | collective-permute-done | bytes 262176 | tf_op jit(solution)/shard_map/while/body/eval_jaxpr/ppermute | solution.py:26
  305.5 26.1 %collective-permute-start = (f32[512,128]{0,1:T(8,128)}, f32[512,128]{0,1:T(8,128)}, u32[]{:S(2)}, u32[]{:S(2)}) collective-permute-start(f32[512,128]{0,1:T(8,128)} %get-tuple-element.479), channel_id=1, source_target_pairs={{1,0},{2,1},{3,2},{4,3},{5,4},{6,5},{7,6},{9,8},{10,9},{11,10},{12... | collective-permute-start | bytes 786440 | tf_op jit(solution)/shard_map/while/body/eval_jaxpr/ppermute | solution.py:26
  334.6 13.7 %collective-permute-done.1 = f32[512,128]{0,1:T(8,128)S(1)} collective-permute-done((f32[512,128]{0,1:T(8,128)}, f32[512,128]{0,1:T(8,128)S(1)}, u32[]{:S(2)}, u32[]{:S(2)}) %collective-permute-start.1) | collective-permute-done | bytes 262176 | tf_op jit(solution)/shard_map/while/body/eval_jaxpr/ppermute | solution.py:26
  348.4 23.0 %collective-permute-start = (f32[512,128]{0,1:T(8,128)}, f32[512,128]{0,1:T(8,128)}, u32[]{:S(2)}, u32[]{:S(2)}) collective-permute-start(f32[512,128]{0,1:T(8,128)} %get-tuple-element.479), channel_id=1, source_target_pairs={{1,0},{2,1},{3,2},{4,3},{5,4},{6,5},{7,6},{9,8},{10,9},{11,10},{12... | collective-permute-start | bytes 786440 | tf_op jit(solution)/shard_map/while/body/eval_jaxpr/ppermute | solution.py:26
  375.0 15.0 %conditional.2 = ((f32[1024,256]{0,1:T(8,128)}, f32[512,128]{0,1:T(8,128)}, f32[512,128]{0,1:T(8,128)})) conditional(s32[]{:T(128)} %convert_element_type.11, (f32[1024,256]{0,1:T(8,128)}, f32[512,128]{0,1:T(8,128)}, f32[512,128]{0,1:T(8,128)}) %tuple.54, (pred[]{:T(512)}, s32[]{:T(128)}, f32[1024,256]{0,1:T(8,128)}, f32[512,128]{0,1:T(8,128)S(1)}, ...), branch_computations={%region_1.1_spmd, %region_2.2_spmd} | conditional | flops 4027383808 | bytes 40108272 | solution.py:100
  376.2 3.0 fusion.3
  380.5 2.3 fusion
  386.0 2.3 constant_dynamic-update-slice_fusion
  390.0 6.2 %collective-permute-start = (f32[512,128]{0,1:T(8,128)}, f32[512,128]{0,1:T(8,128)}, u32[]{:S(2)}, u32[]{:S(2)}) collective-permute-start(f32[512,128]{0,1:T(8,128)} %get-tuple-element.479), channel_id=1, source_target_pairs={{1,0},{2,1},{3,2},{4,3},{5,4},{6,5},{7,6},{9,8},{10,9},{11,10},{12... | collective-permute-start | bytes 786440 | tf_op jit(solution)/shard_map/while/body/eval_jaxpr/ppermute | solution.py:26
  399.9 15.0 %conditional.2 = ((f32[1024,256]{0,1:T(8,128)}, f32[512,128]{0,1:T(8,128)}, f32[512,128]{0,1:T(8,128)})) conditional(s32[]{:T(128)} %convert_element_type.11, (f32[1024,256]{0,1:T(8,128)}, f32[512,128]{0,1:T(8,128)}, f32[512,128]{0,1:T(8,128)}) %tuple.54, (pred[]{:T(512)}, s32[]{:T(128)}, f32[1024,256]{0,1:T(8,128)}, f32[512,128]{0,1:T(8,128)S(1)}, ...), branch_computations={%region_1.1_spmd, %region_2.2_spmd} | conditional | flops 4027383808 | bytes 40108272 | solution.py:100
  401.0 3.0 fusion.3
  405.3 2.3 fusion
  410.8 2.3 constant_dynamic-update-slice_fusion
  414.9 2.0 collective-permute-start
  420.5 2.5 copy.9
  (85 shorter events, 54.2 us)
Async XLA Ops:
  4.9 17.6 %copy-start.5 = (f32[1024,256]{1,0:T(8,128)S(1)}, f32[1024,256]{1,0:T(8,128)}, u32[]{:S(2)}) copy-start(f32[1024,256]{1,0:T(8,128)} %param.7) | copy-start | bytes 3145732
  4.9 170.4 %all-to-all-start = ((f32[64,8,3072]{2,1,0:T(8,128)}), f32[64,8,3072]{2,1,0:T(8,128)}, u32[]{:S(2)}, u32[]{:S(2)}) async-start(f32[64,8,3072]{2,1,0:T(8,128)} %stack.8), calls=%async_computation | async-start | bytes 12582912 | tf_op jit(solution)/shard_map/all_to_all | solution.py:12
  189.1 2.8 copy-start.4
  195.2 4.9 %collective-permute-start = (f32[512,128]{0,1:T(8,128)}, f32[512,128]{0,1:T(8,128)}, u32[]{:S(2)}, u32[]{:S(2)}) collective-permute-start(f32[512,128]{0,1:T(8,128)} %get-tuple-element.479), channel_id=1, source_target_pairs={{1,0},{2,1},{3,2},{4,3},{5,4},{6,5},{7,6},{9,8},{10,9},{11,10},{12... | collective-permute-start | bytes 786440 | tf_op jit(solution)/shard_map/while/body/eval_jaxpr/ppermute | solution.py:26
  198.8 3.6 collective-permute-start.1
  202.4 7.5 %collective-permute-start = (f32[512,128]{0,1:T(8,128)}, f32[512,128]{0,1:T(8,128)}, u32[]{:S(2)}, u32[]{:S(2)}) collective-permute-start(f32[512,128]{0,1:T(8,128)} %get-tuple-element.479), channel_id=1, source_target_pairs={{1,0},{2,1},{3,2},{4,3},{5,4},{6,5},{7,6},{9,8},{10,9},{11,10},{12... | collective-permute-start | bytes 786440 | tf_op jit(solution)/shard_map/while/body/eval_jaxpr/ppermute | solution.py:26
  208.6 14.1 %collective-permute-start.1 = (f32[512,128]{0,1:T(8,128)}, f32[512,128]{0,1:T(8,128)S(1)}, u32[]{:S(2)}, u32[]{:S(2)}) collective-permute-start(f32[512,128]{0,1:T(8,128)} %get-tuple-element.478), channel_id=1, source_target_pairs={{0,1},{1,2},{2,3},{3,4},{4,5},{5,6},{6,7},{8,9},{9,10},{10,11},{11... | collective-permute-start | bytes 786440 | tf_op jit(solution)/shard_map/while/body/eval_jaxpr/ppermute | solution.py:26
  222.7 11.7 %collective-permute-start = (f32[512,128]{0,1:T(8,128)}, f32[512,128]{0,1:T(8,128)}, u32[]{:S(2)}, u32[]{:S(2)}) collective-permute-start(f32[512,128]{0,1:T(8,128)} %get-tuple-element.479), channel_id=1, source_target_pairs={{1,0},{2,1},{3,2},{4,3},{5,4},{6,5},{7,6},{9,8},{10,9},{11,10},{12... | collective-permute-start | bytes 786440 | tf_op jit(solution)/shard_map/while/body/eval_jaxpr/ppermute | solution.py:26
  233.1 3.6 collective-permute-start.1
  236.7 7.6 %collective-permute-start = (f32[512,128]{0,1:T(8,128)}, f32[512,128]{0,1:T(8,128)}, u32[]{:S(2)}, u32[]{:S(2)}) collective-permute-start(f32[512,128]{0,1:T(8,128)} %get-tuple-element.479), channel_id=1, source_target_pairs={{1,0},{2,1},{3,2},{4,3},{5,4},{6,5},{7,6},{9,8},{10,9},{11,10},{12... | collective-permute-start | bytes 786440 | tf_op jit(solution)/shard_map/while/body/eval_jaxpr/ppermute | solution.py:26
  243.0 3.6 collective-permute-start.1
  246.7 7.6 %collective-permute-start = (f32[512,128]{0,1:T(8,128)}, f32[512,128]{0,1:T(8,128)}, u32[]{:S(2)}, u32[]{:S(2)}) collective-permute-start(f32[512,128]{0,1:T(8,128)} %get-tuple-element.479), channel_id=1, source_target_pairs={{1,0},{2,1},{3,2},{4,3},{5,4},{6,5},{7,6},{9,8},{10,9},{11,10},{12... | collective-permute-start | bytes 786440 | tf_op jit(solution)/shard_map/while/body/eval_jaxpr/ppermute | solution.py:26
  252.9 10.4 %collective-permute-start.1 = (f32[512,128]{0,1:T(8,128)}, f32[512,128]{0,1:T(8,128)S(1)}, u32[]{:S(2)}, u32[]{:S(2)}) collective-permute-start(f32[512,128]{0,1:T(8,128)} %get-tuple-element.478), channel_id=1, source_target_pairs={{0,1},{1,2},{2,3},{3,4},{4,5},{5,6},{6,7},{8,9},{9,10},{10,11},{11... | collective-permute-start | bytes 786440 | tf_op jit(solution)/shard_map/while/body/eval_jaxpr/ppermute | solution.py:26
  263.3 29.7 %collective-permute-start = (f32[512,128]{0,1:T(8,128)}, f32[512,128]{0,1:T(8,128)}, u32[]{:S(2)}, u32[]{:S(2)}) collective-permute-start(f32[512,128]{0,1:T(8,128)} %get-tuple-element.479), channel_id=1, source_target_pairs={{1,0},{2,1},{3,2},{4,3},{5,4},{6,5},{7,6},{9,8},{10,9},{11,10},{12... | collective-permute-start | bytes 786440 | tf_op jit(solution)/shard_map/while/body/eval_jaxpr/ppermute | solution.py:26
  291.8 13.8 %collective-permute-start.1 = (f32[512,128]{0,1:T(8,128)}, f32[512,128]{0,1:T(8,128)S(1)}, u32[]{:S(2)}, u32[]{:S(2)}) collective-permute-start(f32[512,128]{0,1:T(8,128)} %get-tuple-element.478), channel_id=1, source_target_pairs={{0,1},{1,2},{2,3},{3,4},{4,5},{5,6},{6,7},{8,9},{9,10},{10,11},{11... | collective-permute-start | bytes 786440 | tf_op jit(solution)/shard_map/while/body/eval_jaxpr/ppermute | solution.py:26
  305.5 27.4 %collective-permute-start = (f32[512,128]{0,1:T(8,128)}, f32[512,128]{0,1:T(8,128)}, u32[]{:S(2)}, u32[]{:S(2)}) collective-permute-start(f32[512,128]{0,1:T(8,128)} %get-tuple-element.479), channel_id=1, source_target_pairs={{1,0},{2,1},{3,2},{4,3},{5,4},{6,5},{7,6},{9,8},{10,9},{11,10},{12... | collective-permute-start | bytes 786440 | tf_op jit(solution)/shard_map/while/body/eval_jaxpr/ppermute | solution.py:26
  331.6 16.8 %collective-permute-start.1 = (f32[512,128]{0,1:T(8,128)}, f32[512,128]{0,1:T(8,128)S(1)}, u32[]{:S(2)}, u32[]{:S(2)}) collective-permute-start(f32[512,128]{0,1:T(8,128)} %get-tuple-element.478), channel_id=1, source_target_pairs={{0,1},{1,2},{2,3},{3,4},{4,5},{5,6},{6,7},{8,9},{9,10},{10,11},{11... | collective-permute-start | bytes 786440 | tf_op jit(solution)/shard_map/while/body/eval_jaxpr/ppermute | solution.py:26
  348.4 24.4 %collective-permute-start = (f32[512,128]{0,1:T(8,128)}, f32[512,128]{0,1:T(8,128)}, u32[]{:S(2)}, u32[]{:S(2)}) collective-permute-start(f32[512,128]{0,1:T(8,128)} %get-tuple-element.479), channel_id=1, source_target_pairs={{1,0},{2,1},{3,2},{4,3},{5,4},{6,5},{7,6},{9,8},{10,9},{11,10},{12... | collective-permute-start | bytes 786440 | tf_op jit(solution)/shard_map/while/body/eval_jaxpr/ppermute | solution.py:26
  371.4 3.6 collective-permute-start.1
  375.0 4.2 copy-start.1
  376.2 4.2 %copy-start = (f32[1024,512]{1,0:T(8,128)S(1)}, f32[1024,512]{1,0:T(8,128)}, u32[]{:S(2)}) copy-start(f32[1024,512]{1,0:T(8,128)} %get-tuple-element.301) | copy-start | bytes 6291460 | tf_op jit(solution)/shard_map/while/body/eval_jaxpr/cond
  383.5 2.5 copy-start.2
  388.3 1.0 copy-start.3
  390.0 7.5 %collective-permute-start = (f32[512,128]{0,1:T(8,128)}, f32[512,128]{0,1:T(8,128)}, u32[]{:S(2)}, u32[]{:S(2)}) collective-permute-start(f32[512,128]{0,1:T(8,128)} %get-tuple-element.479), channel_id=1, source_target_pairs={{1,0},{2,1},{3,2},{4,3},{5,4},{6,5},{7,6},{9,8},{10,9},{11,10},{12... | collective-permute-start | bytes 786440 | tf_op jit(solution)/shard_map/while/body/eval_jaxpr/ppermute | solution.py:26
  396.2 3.6 collective-permute-start.1
  399.9 4.2 copy-start.1
  401.0 4.2 %copy-start = (f32[1024,512]{1,0:T(8,128)S(1)}, f32[1024,512]{1,0:T(8,128)}, u32[]{:S(2)}) copy-start(f32[1024,512]{1,0:T(8,128)} %get-tuple-element.301) | copy-start | bytes 6291460 | tf_op jit(solution)/shard_map/while/body/eval_jaxpr/cond
  408.3 2.5 copy-start.2
  413.1 1.0 copy-start.3
  414.9 3.3 collective-permute-start
  416.9 3.6 collective-permute-start.1
